TPU v7x, 16 devices: a 4x2x1 block of a 4x4x8 slice. The times are simulated.
16 devices in a mesh: data: 2 (over y, z), sp: 8 (over x, core).
Axes of the slice: x: 4, y: 2, z: 1, core: 2. Of those that a mesh axis runs over, the one named last changes fastest.
The devices are a block of a 4x4x8 slice.
Arguments:
- latent: bfloat16 [2, 128, 512, 1152], P('data', 'sp'), parts along dimension 0
- ln_gain: bfloat16 [4, 1152], replicated
- ln_bias: bfloat16 [4, 1152], replicated
- w_qkv: bfloat16 [2, 1152, 3, 16, 72], replicated
- w_out: bfloat16 [2, 16, 72, 1152], replicated
- w_up: bfloat16 [2, 1152, 4608], replicated
- w_down: bfloat16 [2, 4608, 1152], replicated
Outputs:
- output: bfloat16 [2, 128, 512, 1152], P('data', 'sp'), parts along dimension 0
There are 2 independent parts. A program takes and returns all parts, laid end to end along the dimension named above; an argument that names none is the same for every part.
All inputs are finite; a program needn't handle non-finite values.
Results may differ from a plain program's by a relative error of at most 0.012557.
Values are sent between devices in bfloat16 or wider.
A program may use at most 768 MiB of HBM per device.

v0:
```python
import jax
import jax.numpy as jnp
from jax import lax
from jax.sharding import PartitionSpec as P, NamedSharding

LN_EPS = 1e-6
SPACE_FORMS = ('btqhk,btphk->bthqp', 'bthqp,btphk->btqhk')
TIME_FORMS = ('bqshk,bpshk->bshqp', 'bshqp,bpshk->bqshk')


def layer_norm(tokens, gain_vec, shift_vec):
    as_float = tokens.astype(jnp.float32)
    mean_val = jnp.mean(as_float, axis=-1, keepdims=True)
    centered = as_float - mean_val
    variance = jnp.mean(centered * centered, axis=-1, keepdims=True)
    normed = centered * lax.rsqrt(variance + LN_EPS) * gain_vec.astype(jnp.float32) + shift_vec.astype(jnp.float32)
    return normed.astype(jnp.bfloat16)


def project_qkv(tokens, gain_vec, shift_vec, w_qkv_blk):
    normed = layer_norm(tokens, gain_vec, shift_vec)
    return jnp.einsum('btsd,dchk->btschk', normed, w_qkv_blk, preferred_element_type=jnp.float32).astype(jnp.bfloat16)


def attend(qkv_all, ein_forms):
    score_scale = qkv_all.shape[-1] ** -0.5
    query_rows = qkv_all[:, :, :, 0]
    key_rows = qkv_all[:, :, :, 1]
    value_rows = qkv_all[:, :, :, 2]
    scores = jnp.einsum(ein_forms[0], query_rows, key_rows, preferred_element_type=jnp.float32) * score_scale
    attn_probs = jax.nn.softmax(scores, axis=-1).astype(jnp.bfloat16)
    return jnp.einsum(ein_forms[1], attn_probs, value_rows, preferred_element_type=jnp.float32).astype(jnp.bfloat16)


def finish_block(tokens, attended, gain_vec, shift_vec, w_out_blk, w_up_blk, w_down_blk):
    projected = jnp.einsum('btshk,hkd->btsd', attended, w_out_blk, preferred_element_type=jnp.float32)
    residual = (tokens.astype(jnp.float32) + projected).astype(jnp.bfloat16)
    normed = layer_norm(residual, gain_vec, shift_vec)
    hidden = jax.nn.gelu(jnp.einsum('btsd,df->btsf', normed, w_up_blk, preferred_element_type=jnp.float32), approximate=True).astype(jnp.bfloat16)
    result = residual.astype(jnp.float32) + jnp.einsum('btsf,fd->btsd', hidden, w_down_blk, preferred_element_type=jnp.float32)
    return result.astype(jnp.bfloat16)


def value_a9(tokens, layer_idx, ein_forms, ln_gain, ln_bias, w_qkv, w_out, w_up, w_down):
    qkv_all = project_qkv(tokens, ln_gain[2 * layer_idx], ln_bias[2 * layer_idx], w_qkv[layer_idx])
    attended = attend(qkv_all, ein_forms)
    return finish_block(tokens, attended, ln_gain[2 * layer_idx + 1], ln_bias[2 * layer_idx + 1], w_out[layer_idx], w_up[layer_idx], w_down[layer_idx])


def solution(mesh):
    act_spec = P('data', 'sp', None, None)

    def local_run(local_latent, ln_gain, ln_bias, w_qkv, w_out, w_up, w_down):
        mixed_act = value_a9(local_latent, 0, SPACE_FORMS, ln_gain, ln_bias, w_qkv, w_out, w_up, w_down)
        mixed_act = lax.all_to_all(mixed_act, 'sp', 2, 1, tiled=True)
        mixed_act = value_a9(mixed_act, 1, TIME_FORMS, ln_gain, ln_bias, w_qkv, w_out, w_up, w_down)
        return lax.all_to_all(mixed_act, 'sp', 1, 2, tiled=True)

    return jax.shard_map(local_run, mesh=mesh, in_specs=(act_spec, P(), P(), P(), P(), P(), P()), out_specs=act_spec, check_vma=False)
```

profile of v0, /device:TPU:113, one launch (start us, length us, event | category | flops | bytes accessed | tf_op | source)
XLA Modules:
  0.0 1593.5 jit_solution(16012875482478351281)
XLA Ops:
  0.0 11.3 convert_reduce_fusion.2
  11.3 8.5 fusion.40
  20.6 86.2 %convert_bitcast_fusion.1 = bf16[1,16,512,3,16,72]{2,5,4,3,1,0:T(8,128)(2,1)} fusion(bf16[1,16,512,1152]{3,2,1,0:T(8,128)(2,1)} %param.7, f32[1152]{0:T(1024)S(1)} %get-tuple-element.11, f32[1152]{0:T(1024)S(1)} %get-tuple-element.22, f32[16,512]{1,0:T(8,128)S(1)} %add_rsqrt_fusion.3, f32[16,512]{1,0:T(8,128)S(1)} %broadcast_multiply_fusion.3, ...), kind=kOutput, calls=%fused_computation.31 | convolution fusion | flops 65314750464 | bytes 83534848 | tf_op jit(solution)/shard_map/btsd,dchk->btschk/dot_general | solution.py:22
  106.8 107.3 %fusion.94 = (f32[16,16,512]{2,1,0:T(8,128)S(1)}, f32[16,16,512,512]{2,3,1,0:T(8,128)}) fusion(bf16[1,16,512,3,16,72]{2,5,4,3,1,0:T(8,128)(2,1)} %convert_bitcast_fusion.1), kind=kOutput, calls=%fused_computation.132 | convolution fusion | flops 9865003008 | bytes 306708480 | tf_op jit(solution)/shard_map/sub | solution.py:31
  214.1 103.6 %convert_reduce_fusion.1 = (f32[16,512]{1,0:T(8,128)S(1)}, bf16[1,16,512,1152]{3,2,1,0:T(8,128)(2,1)}) fusion(bf16[2,16,72,1152]{3,2,1,0:T(8,128)(2,1)} %param.11, f32[16,16,512,512]{2,3,1,0:T(8,128)} %get-tuple-element.14, f32[16,16,512]{2,1,0:T(8,128)S(1)} %get-tuple-element.13, bf16[1,16,512,3,16,72]{2,5,4,3,1,0:T(8,128)(2,1)} %convert_bitcast_fusion.1, ...), kind=kOutput, calls=%fused_computation.37 | convolution fusion | flops 31597780992 | bytes 328269824 | tf_op jit(solution)/shard_map/btshk,hkd->btsd/dot_general | solution.py:36
  317.6 8.5 fusion.36
  326.2 19.0 %fusion.129 = bf16[16,512,1152]{2,1,0:T(8,128)(2,1)} fusion(bf16[1,16,512,1152]{3,2,1,0:T(8,128)(2,1)} %get-tuple-element.16, f32[1152]{0:T(1024)S(1)} %copy-done.6, f32[1152]{0:T(1024)S(1)} %copy-done.7, f32[16,512]{1,0:T(8,128)S(1)} %add_rsqrt_fusion.2, f32[16,512]{1,0:T(8,128)S(1)} %broadcast_multiply_fusion.2), kind=kLoop, calls=%fused_computation.72.clone.clone.2 | loop fusion | flops 56623104 | bytes 37823488 | tf_op jit(solution)/shard_map/btsd,df->btsf/dot_general | solution.py:39
  345.2 127.6 %fusion.12 = bf16[16,512,4608]{2,1,0:T(8,128)(2,1)} fusion(bf16[2,1152,4608]{2,1,0:T(8,128)(2,1)} %param.12, bf16[16,512,1152]{2,1,0:T(8,128)(2,1)} %fusion.129), kind=kOutput, calls=%fused_computation.15 | convolution fusion | flops 87312826368 | bytes 104988672 | tf_op jit(solution)/shard_map/btsd,df->btsf/dot_general | solution.py:39
  472.8 116.7 %fusion.45 = bf16[1,16,512,1152]{3,2,1,0:T(8,128)(2,1)} fusion(bf16[1,16,512,1152]{3,2,1,0:T(8,128)(2,1)} %get-tuple-element.16, bf16[16,512,4608]{2,1,0:T(8,128)(2,1)} %fusion.12, bf16[2,4608,1152]{2,1,0:T(8,128)(2,1)} %param.13), kind=kOutput, calls=%fused_computation.60 | convolution fusion | flops 87001399296 | bytes 123863040 | tf_op jit(solution)/shard_map/btsf,fd->btsd/dot_general | solution.py:40
  589.5 16.3 %copy.14 = bf16[1,16,512,1152]{3,1,0,2:T(8,128)(2,1)S(1)} copy(bf16[1,16,512,1152]{3,2,1,0:T(8,128)(2,1)} %fusion.45) | data formatting | bytes 37748736 | tf_op jit(solution)/shard_map/convert_element_type | solution.py:41
  605.9 211.8 %all_to_all.27 = bf16[1,16,512,1152]{3,1,0,2:T(8,128)(2,1)S(1)} all-to-all(bf16[1,16,512,1152]{3,1,0,2:T(8,128)(2,1)S(1)} %copy.14), channel_id=1, replica_groups=mesh['data'=2,'sp'=8] {'sp'}, dimensions={2} | all-to-all | bytes 37748736 | tf_op jit(solution)/shard_map/all_to_all | solution.py:55
  817.7 10.8 bitcast_reduce_fusion
  828.5 12.9 copy.15
  847.7 11.0 add_convert_fusion
  858.7 81.5 %convert_bitcast_fusion = bf16[1,128,64,3,16,72]{1,5,4,3,2,0:T(8,128)(2,1)} fusion(bf16[128,64,1152,1,1]{2,0,4,3,1:T(8,128)(2,1)} %bitcast.206, bf16[2,1152,3,16,72]{1,4,3,2,0:T(8,128)(2,1)S(1)} %bitcast.208), kind=kOutput, calls=%fused_computation.30 | convolution fusion | flops 65258127360 | bytes 83460096 | tf_op jit(solution)/shard_map/btsd,dchk->btschk/dot_general | solution.py:22
  940.2 34.8 %fusion.57 = f32[64,16,128,128]{2,3,1,0:T(8,128)} fusion(bf16[1,128,64,3,16,72]{1,5,4,3,2,0:T(8,128)(2,1)} %convert_bitcast_fusion), kind=kOutput, calls=%fused_computation.74 | convolution fusion | flops 2415919104 | bytes 104857600 | tf_op jit(solution)/shard_map/bqshk,bpshk->bshqp/dot_general | solution.py:30
  975.0 68.4 %fusion.95 = (f32[64,16,128]{2,1,0:T(8,128)S(1)}, f32[64,16,128,128]{2,3,1,0:T(8,128)}) fusion(f32[64,16,128,128]{2,3,1,0:T(8,128)} %fusion.57), kind=kOutput, calls=%fused_computation.133 | output fusion | flops 67108992 | bytes 134742016 | tf_op jit(solution)/shard_map/sub | solution.py:31
  1043.3 53.1 %convert_reduce_fusion = (f32[128,64]{0,1:T(8,128)S(1)}, bf16[128,64,1152]{2,0,1:T(8,128)(2,1)}) fusion(f32[128,64,1152]{2,0,1:T(8,128)} %bitcast.205, bf16[2,16,72,1152]{3,2,1,0:T(8,128)(2,1)} %param.11, f32[64,16,128,128]{2,3,1,0:T(8,128)} %get-tuple-element.18, f32[64,16,128]{2,1,0:T(8,128)S(1)} %get-tuple-element.17, ...), kind=kOutput, calls=%fused_computation.34 | convolution fusion | flops 24239923200 | bytes 145817600 | tf_op jit(solution)/shard_map/btshk,hkd->btsd/dot_general | solution.py:36
  1096.5 8.5 fusion.32
  1105.0 19.2 %fusion.131 = bf16[128,64,1152]{2,0,1:T(8,128)(2,1)} fusion(bf16[128,64,1152]{2,0,1:T(8,128)(2,1)} %get-tuple-element.20, f32[1152]{0:T(1024)S(1)} %copy-done.2, f32[1152]{0:T(1024)S(1)} %copy-done.3, f32[128,64]{0,1:T(8,128)S(1)} %add_rsqrt_fusion.1, f32[128,64]{0,1:T(8,128)S(1)} %broadcast_multiply_fusion.1), kind=kLoop, calls=%fused_computation.50.clone.clone.2 | loop fusion | flops 56623104 | bytes 37823488 | tf_op jit(solution)/shard_map/btsd,df->btsf/dot_general | solution.py:39
  1124.2 127.9 %fusion.20 = bf16[128,64,4608]{2,0,1:T(8,128)(2,1)} fusion(bf16[2,1152,4608]{2,1,0:T(8,128)(2,1)} %param.12, bf16[128,64,1152]{2,0,1:T(8,128)(2,1)} %fusion.131), kind=kOutput, calls=%fused_computation.23 | convolution fusion | flops 87312826368 | bytes 104988672 | tf_op jit(solution)/shard_map/btsd,df->btsf/dot_general | solution.py:39
  1252.0 107.9 %fusion.75 = bf16[1,128,64,1152]{3,1,2,0:T(8,128)(2,1)} fusion(bf16[128,64,4608]{2,0,1:T(8,128)(2,1)} %fusion.20, bf16[128,64,1152]{2,0,1:T(8,128)(2,1)} %get-tuple-element.20, bf16[2,4608,1152]{2,1,0:T(8,128)(2,1)} %param.13), kind=kOutput, calls=%fused_computation.97 | convolution fusion | flops 87001399296 | bytes 123863040 | tf_op jit(solution)/shard_map/btsf,fd->btsd/dot_general | solution.py:40
  1359.9 16.3 %copy.17 = bf16[1,128,64,1152]{3,2,0,1:T(8,128)(2,1)S(1)} copy(bf16[1,128,64,1152]{3,1,2,0:T(8,128)(2,1)} %fusion.75) | data formatting | bytes 37748736 | tf_op jit(solution)/shard_map/convert_element_type | solution.py:41
  1376.3 210.0 %all_to_all.28 = bf16[1,128,64,1152]{3,2,0,1:T(8,128)(2,1)S(1)} all-to-all(bf16[1,128,64,1152]{3,2,0,1:T(8,128)(2,1)S(1)} %copy.17), channel_id=1, replica_groups=mesh['data'=2,'sp'=8] {'sp'}, dimensions={1} | all-to-all | bytes 37748736 | tf_op jit(solution)/shard_map/all_to_all | solution.py:57
  (36 shorter events, 13.9 us)
Async XLA Ops:
  0.0 19.9 %copy-start = (bf16[4,1152]{1,0:T(4,128)(2,1)S(1)}, bf16[4,1152]{1,0:T(4,128)(2,1)}, u32[]{:S(2)}) copy-start(bf16[4,1152]{1,0:T(4,128)(2,1)} %param.9) | copy-start | bytes 27652
  0.0 19.9 %copy-start.1 = (bf16[4,1152]{1,0:T(4,128)(2,1)S(1)}, bf16[4,1152]{1,0:T(4,128)(2,1)}, u32[]{:S(2)}) copy-start(bf16[4,1152]{1,0:T(4,128)(2,1)} %param.8) | copy-start | bytes 27652
  214.1 112.1 %copy-start.6 = (f32[1152]{0:T(1024)S(1)}, f32[1152]{0:T(1024)}, u32[]{:S(2)}) copy-start(f32[1152]{0:T(1024)} %get-tuple-element.10) | copy-start | bytes 13828
  214.1 112.1 %copy-start.7 = (f32[1152]{0:T(1024)S(1)}, f32[1152]{0:T(1024)}, u32[]{:S(2)}) copy-start(f32[1152]{0:T(1024)} %get-tuple-element.23) | copy-start | bytes 13828
  828.5 19.2 %copy-start.4 = (f32[1152]{0:T(1024)S(1)}, f32[1152]{0:T(1024)}, u32[]{:S(2)}) copy-start(f32[1152]{0:T(1024)} %get-tuple-element.12) | copy-start | bytes 13828
  828.5 19.2 %copy-start.5 = (f32[1152]{0:T(1024)S(1)}, f32[1152]{0:T(1024)}, u32[]{:S(2)}) copy-start(f32[1152]{0:T(1024)} %get-tuple-element.21) | copy-start | bytes 13828
  841.4 17.3 %slice-start = ((s8[15925248]{0:T(1024)(128)(4,1)}), s8[4194304]{0:T(1024)(128)(4,1)S(1)}, s32[]{:S(2)}) async-start(s8[15925248]{0:T(1024)(128)(4,1)} %bitcast.207), calls=%async_computation.2 | async-start | bytes 8388608
  841.4 17.3 %slice-start.1 = ((s8[15925248]{0:T(1024)(128)(4,1)}), s8[4194304]{0:T(1024)(128)(4,1)S(1)}, s32[]{:S(2)}) async-start(s8[15925248]{0:T(1024)(128)(4,1)} %bitcast.207), calls=%async_computation.3 | async-start | bytes 8388608
  847.7 11.0 slice-start.2
  847.7 11.0 slice-start.3
  1043.3 61.6 %copy-start.2 = (f32[1152]{0:T(1024)S(1)}, f32[1152]{0:T(1024)}, u32[]{:S(2)}) copy-start(f32[1152]{0:T(1024)} %get-tuple-element.9) | copy-start | bytes 13828
  1043.3 61.6 %copy-start.3 = (f32[1152]{0:T(1024)S(1)}, f32[1152]{0:T(1024)}, u32[]{:S(2)}) copy-start(f32[1152]{0:T(1024)} %get-tuple-element.24) | copy-start | bytes 13828
where the time goes:
time: 1600 us; the launch traced here: 1590 us
  matrix products  947 us (59%)
  blocking collectives  422 us (26%)
  other arithmetic  172 us (11%)
  local copies, waits for them, and re-layouts  52.5 us (3%)
    dot_general x2, matrix products, finish_block(): jnp.einsum('btsd,df->btsf', normed, w_up_blk, preferred_element_type=jnp....  256 us
    dot_general x2, matrix products, finish_block(): jnp.einsum('btsf,fd->btsd', hidden, w_down_blk, preferred_element_type=jn...  225 us
    all_to_all x1, blocking collectives, local_run(): mixed_act = lax.all_to_all(mixed_act, 'sp', 2, 1, tiled=True)  212 us
    all_to_all x1, blocking collectives, local_run(): return lax.all_to_all(mixed_act, 'sp', 1, 2, tiled=True)  210 us
    dot_general x2, matrix products, project_qkv(): jnp.einsum('btsd,dchk->btschk', normed, w_qkv_blk, preferred_element_type...  168 us
    dot_general x2, matrix products, finish_block(): jnp.einsum('btshk,hkd->btsd', attended, w_out_blk, preferred_element_type...  157 us
    sub x1, matrix products, attend(): attn_probs = jax.nn.softmax(scores, axis=-1).astype(jnp.bfloat16)  107 us
    sub x1, other arithmetic, attend(): attn_probs = jax.nn.softmax(scores, axis=-1).astype(jnp.bfloat16)  68.4 us

commit v1 on v0

v1 whole, which is shorter than its diff:
```python
import functools

import jax
import jax.numpy as jnp
from jax import lax
from jax.experimental import pallas as pl
from jax.experimental.pallas import tpu as pltpu
from jax.sharding import PartitionSpec as P

BF, F32 = jnp.bfloat16, jnp.float32
LN_EPS = 1e-6
LOG2E = 1.4426950408889634
LANES = 128
WIN = 2 * LANES
GROUP = 8
MESH = pl.DeviceIdType.MESH
VMEM_LIMIT = 66_000_000


def layer_norm(x, gain, bias):
    mean = jnp.mean(x, axis=-1, keepdims=True)
    c = x - mean
    var = jnp.mean(c * c, axis=-1, keepdims=True)
    return (c * lax.rsqrt(var + LN_EPS) * gain + bias).astype(BF)


def gelu(x):
    return 0.5 * x * (1.0 + jnp.tanh(0.7978845608028654 * (x + 0.044715 * (x * x * x))))


def dot(a, b):
    return jnp.dot(a, b, preferred_element_type=F32)


def dot_nt(a, b):
    return lax.dot_general(a, b, (((1,), (1,)), ((), ())), preferred_element_type=F32)


def softmax_rows(s, scale):
    m = jnp.max(s, axis=-1, keepdims=True)
    e = jnp.exp2((s - m) * (scale * LOG2E))
    return (e * (1.0 / jnp.sum(e, axis=-1, keepdims=True))).astype(BF)


def head_masks(j, hd):
    lane = lax.broadcasted_iota(jnp.int32, (1, WIN), 1)
    lo = j * (2 * hd - LANES)
    return [jnp.where((lane >= lo + i * hd) & (lane < lo + (i + 1) * hd), 1.0, 0.0).astype(BF) for i in range(2)]


def params(gain_ref, bias_ref, row):
    return gain_ref[row:row + 1, :].astype(F32), bias_ref[row:row + 1, :].astype(F32)


def greet(axis, n):
    me = lax.axis_index(axis)
    barrier = pltpu.get_barrier_semaphore()
    for r in range(1, n):
        pl.semaphore_signal(barrier, inc=1, device_id={axis: lax.rem(me + r, n)}, device_id_type=MESH)
    pl.semaphore_wait(barrier, n - 1)


def weight_copies(layer, srcs, dsts, sems):
    return [pltpu.make_async_copy(s.at[layer], d, sems.at[i]) for i, (s, d) in enumerate(zip(srcs, dsts))]


def spatial_kernel(hd, n, axis, x_ref, gain_ref, bias_ref, wqkv_h, wout_h, wup_h, wdown_h, recv_ref,
                   wqkv, wout, wup, wdown, a_ref, qkv_ref, o_ref, h_ref, hid_ref, y_ref,
                   w_sem, send_sem, recv_sem, own_sem):
    frames = pl.num_programs(0)
    step = pl.program_id(0)
    _, T, C = x_ref.shape
    share = T // n
    scale = hd ** -0.5
    me = lax.axis_index(axis)
    slot = lax.rem(step, 2)
    cps = weight_copies(0, (wqkv_h, wout_h, wup_h, wdown_h), (wqkv, wout, wup, wdown), w_sem)

    def send(r, sl, frame):
        peer = lax.rem(me + r, n)
        return pltpu.make_async_remote_copy(
            src_ref=y_ref.at[sl, pl.ds(pl.multiple_of(peer * share, share), share)],
            dst_ref=recv_ref.at[me * frames + frame],
            send_sem=send_sem.at[sl, r], recv_sem=recv_sem.at[r],
            device_id={axis: peer}, device_id_type=MESH)

    def keep(sl, frame):
        return pltpu.make_async_copy(y_ref.at[sl, pl.ds(pl.multiple_of(me * share, share), share)],
                                     recv_ref.at[me * frames + frame], own_sem.at[sl])

    @pl.when(step == 0)
    def _():
        for c in cps:
            c.start()

    a_ref[...] = layer_norm(x_ref[0].astype(F32), *params(gain_ref, bias_ref, 0))

    @pl.when(step == 0)
    def _():
        greet(axis, n)
        cps[0].wait()

    qkv_ref[...] = dot(a_ref[...], wqkv[...]).astype(BF)
    o_ref[:, 0:LANES] = jnp.zeros((T, LANES), BF)
    for j in range(C // (2 * hd)):
        c0 = j * LANES
        q, k, v = (qkv_ref[:, pl.ds(i * C + c0, WIN)] for i in range(3))
        o = sum(dot(softmax_rows(dot_nt(q, k * m), scale), v * m) for m in head_masks(j, hd)).astype(BF)
        o_ref[:, pl.ds(c0, LANES)] = o_ref[:, pl.ds(c0, LANES)] + o[:, :LANES]
        o_ref[:, pl.ds(c0 + LANES, LANES)] = o[:, LANES:]

    @pl.when(step == 0)
    def _():
        for c in cps[1:]:
            c.wait()

    @pl.when(step >= 2)
    def _():
        for r in range(1, n):
            send(r, slot, step - 2).wait_send()
        keep(slot, step - 2).wait()

    h = (x_ref[0].astype(F32) + dot(o_ref[...], wout[...])).astype(BF)
    h_ref[...] = h
    a_ref[...] = layer_norm(h.astype(F32), *params(gain_ref, bias_ref, 1))
    hid_ref[...] = gelu(dot(a_ref[...], wup[...])).astype(BF)
    y_ref[slot] = (h_ref[...].astype(F32) + dot(hid_ref[...], wdown[...])).astype(BF)
    for r in range(1, n):
        send(r, slot, step).start()
    keep(slot, step).start()

    @pl.when(step == frames - 1)
    def _():
        for sl, frame in ((1 - slot, step - 1), (slot, step)):
            for r in range(1, n):
                send(r, sl, frame).wait_send()
            keep(sl, frame).wait()
        for r in range(1, n):
            src = lax.rem(me + n - r, n)
            block = recv_ref.at[pl.ds(src * frames, frames)]
            pltpu.make_async_remote_copy(src_ref=block, dst_ref=block, send_sem=send_sem.at[0, r],
                                         recv_sem=recv_sem.at[r], device_id={axis: src},
                                         device_id_type=MESH).wait_recv()


def get_rows(ref, part, d):
    return jnp.concatenate([ref[part, i, d, :] for i in range(ref.shape[1])], axis=1)


def put_rows(ref, part, d, val):
    for i in range(ref.shape[1]):
        ref[part, i, d, :] = val[:, i * LANES:(i + 1) * LANES]


def temporal_kernel(hd, n, axis, x_ref, gain_ref, bias_ref, wqkv_h, wout_h, wup_h, wdown_h, out_ref,
                    wqkv, wout, wup, wdown, xs_ref, a_ref, qkv_ref, o_ref, h_ref, hid_ref, y_ref,
                    w_sem, send_sem, recv_sem, own_sem):
    steps = pl.num_programs(0)
    step = pl.program_id(0)
    F, G, C = x_ref.shape
    mine = F // n
    half = F // 2
    rows = half * G
    scale = hd ** -0.5
    me = lax.axis_index(axis)
    per = n // 2
    base = lax.div(me, per)
    cps = weight_copies(1, (wqkv_h, wout_h, wup_h, wdown_h), (wqkv, wout, wup, wdown), w_sem)

    def place(ref, who, st):
        return ref.at[:, pl.ds(pl.multiple_of(who * (steps * G) + st * G, G), G), :]

    def send(part, r, st):
        inner = lax.rem(me + r, per)
        peer = (1 - base if part == 0 else base) * per + inner
        return pltpu.make_async_remote_copy(
            src_ref=y_ref.at[part, pl.ds(inner * mine, mine)], dst_ref=place(out_ref, me, st),
            send_sem=send_sem.at[part, r], recv_sem=recv_sem.at[part, r],
            device_id={axis: peer}, device_id_type=MESH)

    def sends(part, st):
        return [send(part, r, st) for r in range(part, per)]

    def keep(st):
        return pltpu.make_async_copy(y_ref.at[1, pl.ds(lax.rem(me, per) * mine, mine)], place(out_ref, me, st),
                                     own_sem.at[0])

    @pl.when(step == 0)
    def _():
        for c in cps:
            c.start()

    for part in range(2):
        put_rows(xs_ref, part, pl.ds(0, rows), x_ref[pl.ds(part * half, half)].astype(F32).reshape(rows, C))
    for p in range(G):
        for part in range(2):
            a_ref[pl.ds(p * F + part * half, half), :] = layer_norm(
                get_rows(xs_ref, part, pl.ds(p, half, stride=G)), *params(gain_ref, bias_ref, 2))

    @pl.when(step == 0)
    def _():
        greet(axis, n)
        cps[0].wait()

    def project(i, _):
        r = pl.ds(pl.multiple_of(i * rows, rows), rows)
        qkv_ref[r, :] = dot(a_ref[r, :], wqkv[...]).astype(BF)
        return 0

    lax.fori_loop(0, 2, project, 0)

    o_ref[:, :, 0:LANES] = jnp.zeros((G, F, LANES), BF)
    for j in range(C // (2 * hd)):
        c0 = j * LANES
        m0, m1 = head_masks(j, hd)
        for p in range(G):
            q, k, v = (qkv_ref[pl.ds(p * F, F), pl.ds(i * C + c0, WIN)] for i in range(3))
            s = dot_nt(q, jnp.concatenate([k * m0, k * m1], axis=0))
            pr = jnp.concatenate([softmax_rows(s[:, :F], scale), softmax_rows(s[:, F:], scale)], axis=1)
            o = dot(pr, jnp.concatenate([v * m0, v * m1], axis=0)).astype(BF)
            o_ref[p, :, pl.ds(c0, LANES)] = o_ref[p, :, pl.ds(c0, LANES)] + o[:, :LANES]
            o_ref[p, :, pl.ds(c0 + LANES, LANES)] = o[:, LANES:]

    @pl.when(step == 0)
    def _():
        for c in cps[1:]:
            c.wait()

    for part in range(2):
        sel = 1 - base if part == 0 else base

        @pl.when(step >= 1)
        def _():
            for c in sends(part, step - 1):
                c.wait_send()
            if part == 1:
                keep(step - 1).wait()

        o = o_ref[:, pl.ds(pl.multiple_of(sel * half, half), half), :].reshape(rows, C)
        x = jnp.concatenate([get_rows(xs_ref, sel, pl.ds(p, half, stride=G)) for p in range(G)], axis=0)
        h = (x + dot(o, wout[...])).astype(BF)
        h_ref[...] = h
        a_ref[pl.ds(0, rows), :] = layer_norm(h.astype(F32), *params(gain_ref, bias_ref, 3))
        hid_ref[...] = gelu(dot(a_ref[pl.ds(0, rows), :], wup[...])).astype(BF)
        y = h_ref[...].astype(F32) + dot(hid_ref[...], wdown[...])
        for p in range(G):
            put_rows(xs_ref, sel, pl.ds(p, half, stride=G), y[p * half:(p + 1) * half])
        y_ref[part] = get_rows(xs_ref, sel, pl.ds(0, rows)).reshape(half, G, C).astype(BF)
        for c in sends(part, step):
            c.start()
        if part == 1:
            keep(step).start()

    @pl.when(step == steps - 1)
    def _():
        for part in range(2):
            for c in sends(part, step):
                c.wait_send()
        keep(step).wait()
        for part in range(2):
            for r in range(part, per):
                src = (1 - base if part == 0 else base) * per + lax.rem(me + per - r, per)
                block = out_ref.at[:, pl.ds(pl.multiple_of(src * (steps * G), steps * G), steps * G), :]
                pltpu.make_async_remote_copy(src_ref=block, dst_ref=block, send_sem=send_sem.at[part, r],
                                             recv_sem=recv_sem.at[part, r], device_id={axis: src},
                                             device_id_type=MESH).wait_recv()


def compiler_params(cid):
    return pltpu.CompilerParams(vmem_limit_bytes=VMEM_LIMIT, dimension_semantics=("arbitrary",), collective_id=cid,
                                has_side_effects=True)


def weight_scratch(C, H):
    return [pltpu.VMEM((C, 3 * C), BF), pltpu.VMEM((C, C), BF), pltpu.VMEM((C, H), BF), pltpu.VMEM((H, C), BF)]


def spatial_block(x, small, weights, hd, n, axis):
    frames, T, C = x.shape
    H = weights[2].shape[-1]
    any_spec = pl.BlockSpec(memory_space=pl.ANY)
    dma = pltpu.SemaphoreType.DMA
    return pl.pallas_call(
        functools.partial(spatial_kernel, hd, n, axis),
        grid=(frames,),
        in_specs=[pl.BlockSpec((1, T, C), lambda i: (i, 0, 0))]
        + [pl.BlockSpec(s.shape, lambda i: (0, 0)) for s in small] + [any_spec] * 4,
        out_specs=any_spec,
        out_shape=jax.ShapeDtypeStruct((n * frames, T // n, C), BF),
        scratch_shapes=weight_scratch(C, H) + [
            pltpu.VMEM((T, C), BF), pltpu.VMEM((T, 3 * C), BF), pltpu.VMEM((T, C), BF), pltpu.VMEM((T, C), BF),
            pltpu.VMEM((T, H), BF), pltpu.VMEM((2, T, C), BF),
            dma((4,)), dma((2, n)), dma((n,)), dma((2,))],
        compiler_params=compiler_params(0),
        name='spatial',
    )(x, *small, *weights)


def temporal_block(x, small, weights, hd, n, axis):
    F, share, C = x.shape
    H = weights[2].shape[-1]
    any_spec = pl.BlockSpec(memory_space=pl.ANY)
    dma = pltpu.SemaphoreType.DMA
    rows = F * GROUP // 2
    return pl.pallas_call(
        functools.partial(temporal_kernel, hd, n, axis),
        grid=(share // GROUP,),
        in_specs=[pl.BlockSpec((F, GROUP, C), lambda i: (0, i, 0))]
        + [pl.BlockSpec(s.shape, lambda i: (0, 0)) for s in small] + [any_spec] * 4,
        out_specs=any_spec,
        out_shape=jax.ShapeDtypeStruct((F // n, share * n, C), BF),
        scratch_shapes=weight_scratch(C, H) + [
            pltpu.VMEM((2, C // LANES, rows, LANES), F32), pltpu.VMEM((2 * rows, C), BF), pltpu.VMEM((2 * rows, 3 * C), BF),
            pltpu.VMEM((GROUP, F, C), BF), pltpu.VMEM((rows, C), BF),
            pltpu.VMEM((rows, H), BF), pltpu.VMEM((2, F // 2, GROUP, C), BF),
            dma((4,)), dma((2, n)), dma((2, n)), dma((1,))],
        compiler_params=compiler_params(1),
        name='temporal',
    )(x, *small, *weights)


def solution(mesh):
    n = mesh.shape['sp']
    act = P('data', 'sp', None, None)

    def local_run(latent, ln_gain, ln_bias, w_qkv, w_out, w_up, w_down):
        L, C, _, heads, hd = w_qkv.shape
        weights = (w_qkv.reshape(L, C, 3 * heads * hd), w_out.reshape(L, heads * hd, C), w_up, w_down)
        small = (ln_gain, ln_bias)
        mixed = spatial_block(latent[0], small, weights, hd, n, 'sp')
        return temporal_block(mixed, small, weights, hd, n, 'sp')[None]

    return jax.shard_map(local_run, mesh=mesh, in_specs=(act, P(), P(), P(), P(), P(), P()), out_specs=act, check_vma=False)
```

time: 1600 us -> 1160 us (0.72)
  Pallas kernels: 0 us -> 1100 us
  matrix products: 947 us -> 0 us
  blocking collectives: 422 us -> 0 us
  other arithmetic: 172 us -> 0 us
    pallas_call x0 -> x2, Pallas kernels: none -> 1100 us  [the longest x1 645 us: temporal_block(): pl.pallas_call(functools.partial(temporal_kernel, hd, n, axis), grid=(sha...]
    dot_general x9 -> x0, matrix products: 839 us -> none  [the longest x2 256 us: finish_block(): jnp.einsum('btsd,df->btsf', normed, w_up_blk, preferred_element_type=jnp....]
    all_to_all x2 -> x0, blocking collectives: 422 us -> none  [the longest x1 212 us: local_run(): mixed_act = lax.all_to_all(mixed_act, 'sp', 2, 1, tiled=True)]
    sub x1 -> x0, matrix products: 107 us -> none  [attend(): attn_probs = jax.nn.softmax(scores, axis=-1).astype(jnp.bfloat16)]
    sub x1 -> x0, other arithmetic: 68.4 us -> none  [attend(): attn_probs = jax.nn.softmax(scores, axis=-1).astype(jnp.bfloat16)]
    reduce_sum x6 -> x0, other arithmetic: 53.7 us -> none  [the longest x4 31.6 us: layer_norm(): variance = jnp.mean(centered * centered, axis=-1, keepdims=True)]
    convert_element_type x3 -> x0, local copies, waits for them, and re-layouts: 45.6 us -> none  [the longest x2 32.7 us: finish_block(): return result.astype(jnp.bfloat16)]
    dot_general x2 -> x0, other arithmetic: 38.2 us -> none  [finish_block(): jnp.einsum('btsd,df->btsf', normed, w_up_blk, preferred_element_type=jnp....]
where the time goes in v1:
time: 1160 us; the launch traced here: 1140 us
  Pallas kernels  1100 us (95%)
  local copies, waits for them, and re-layouts  37.3 us (3%)
    pallas_call x1, Pallas kernels, temporal_block(): pl.pallas_call(functools.partial(temporal_kernel, hd, n, axis), grid=(sha...  645 us
    pallas_call x1, Pallas kernels, spatial_block(): pl.pallas_call(functools.partial(spatial_kernel, hd, n, axis), grid=(fram...  458 us

profile of v1, /device:TPU:113, one launch (start us, length us, event | category | flops | bytes accessed | tf_op | source)
XLA Modules:
  0.0 1141.4 jit_solution(14150694737400096789)
XLA Ops:
  0.0 20.6 %copy.9.wqkv_h = bf16[2,1152,3456]{2,1,0:T(8,128)(2,1)} copy(bf16[2,1152,3456]{1,2,0:T(8,128)(2,1)} %bitcast.8) | data formatting | bytes 31850496 | tf_op jit(solution)/shard_map/reshape | solution.py:328
  20.6 458.3 %spatial.1.x_ref = bf16[128,64,1152]{2,1,0:T(8,128)(2,1)} custom-call(bf16[16,512,1152]{2,1,0:T(8,128)(2,1)} %bitcast.7, bf16[4,1152]{1,0:T(4,128)(2,1)} %gain_ref.3, bf16[4,1152]{1,0:T(4,128)(2,1)} %bias_ref.3, bf16[2,1152,3456]{2,1,0:T(8,128)(2,1)} %copy.9.wqkv_h, bf16[2,1152,1152]{2,1,0:T(8,128)(2,1)} %bitcast.5, bf16[2,1152,4608]{2,1,0:T(8,128)(2,1)} %wup_h.3, ...), custom_call_target="tpu_custom_call" | custom-call | tf_op jit(solution)/shard_map/spatial/pallas_call | solution.py:283
  478.9 645.2 %temporal.1 = bf16[16,512,1152]{2,1,0:T(8,128)(2,1)} custom-call(bf16[128,64,1152]{2,1,0:T(8,128)(2,1)} %spatial.1.x_ref, bf16[4,1152]{1,0:T(4,128)(2,1)} %gain_ref.3, bf16[4,1152]{1,0:T(4,128)(2,1)} %bias_ref.3, bf16[2,1152,3456]{2,1,0:T(8,128)(2,1)} %copy.9.wqkv_h, bf16[2,1152,1152]{2,1,0:T(8,128)(2,1)} %bitcast.6, bf16[2,1152,4608]{2,1,0:T(8,128)(2,1)} %wup_h.3, ...), custom_call_target="tpu_custom_call" | custom-call | tf_op jit(solution)/shard_map/temporal/pallas_call | solution.py:305
  1124.1 16.7 %copy.12 = bf16[1,16,512,1152]{3,2,1,0:T(8,128)(2,1)} copy(bf16[1,16,512,1152]{3,2,1,0:T(8,128)(2,1)} %bitcast.4) | data formatting | bytes 37748736

commit v2 on v1

--- a/solution.py
+++ b/solution.py
@@ -40,6 +40,10 @@
     m = jnp.max(s, axis=-1, keepdims=True)
     e = jnp.exp2((s - m) * (scale * LOG2E))
     return (e * (1.0 / jnp.sum(e, axis=-1, keepdims=True))).astype(BF)
+
+
+def exp_rows(s, scale):
+    return jnp.exp2((s - jnp.max(s, axis=-1, keepdims=True)) * (scale * LOG2E)).astype(BF)
 
 
 def head_masks(j, hd):
@@ -210,16 +214,36 @@
     lax.fori_loop(0, 2, project, 0)
 
     o_ref[:, :, 0:LANES] = jnp.zeros((G, F, LANES), BF)
-    for j in range(C // (2 * hd)):
+
+    def scores(j):
+        m0, m1 = head_masks(j, hd)
+        out = []
+        for p in range(G):
+            q, k = (qkv_ref[pl.ds(p * F, F), pl.ds(i * C + j * LANES, WIN)] for i in range(2))
+            out.append(dot_nt(q, jnp.concatenate([k * m0, k * m1], axis=0)))
+        return out
+
+    def weigh(j, ss):
         c0 = j * LANES
         m0, m1 = head_masks(j, hd)
+        tally = jnp.concatenate([jnp.broadcast_to(m0, (F, WIN)), jnp.broadcast_to(1 - m0, (F, WIN))], axis=0)
+        es = [jnp.concatenate([exp_rows(s[:, :F], scale), exp_rows(s[:, F:], scale)], axis=1) for s in ss]
+        nums, dens = [], []
         for p in range(G):
-            q, k, v = (qkv_ref[pl.ds(p * F, F), pl.ds(i * C + c0, WIN)] for i in range(3))
-            s = dot_nt(q, jnp.concatenate([k * m0, k * m1], axis=0))
-            pr = jnp.concatenate([softmax_rows(s[:, :F], scale), softmax_rows(s[:, F:], scale)], axis=1)
-            o = dot(pr, jnp.concatenate([v * m0, v * m1], axis=0)).astype(BF)
+            v = qkv_ref[pl.ds(p * F, F), pl.ds(2 * C + c0, WIN)]
+            nums.append(dot(es[p], jnp.concatenate([v * m0, v * m1], axis=0)))
+            dens.append(dot(es[p], tally))
+        for p in range(G):
+            o = (nums[p] / dens[p]).astype(BF)
             o_ref[p, :, pl.ds(c0, LANES)] = o_ref[p, :, pl.ds(c0, LANES)] + o[:, :LANES]
             o_ref[p, :, pl.ds(c0 + LANES, LANES)] = o[:, LANES:]
+
+    pairs = C // (2 * hd)
+    held = scores(0)
+    for j in range(pairs):
+        following = scores(j + 1) if j + 1 < pairs else None
+        weigh(j, held)
+        held = following
 
     @pl.when(step == 0)
     def _():

time: 1160 us -> 1000 us (0.86)
  Pallas kernels: 1100 us -> 947 us
    pallas_call x1, Pallas kernels: 645 us -> 488 us  [temporal_block(): pl.pallas_call(functools.partial(temporal_kernel, hd, n, axis), grid=(sha...]
where the time goes in v2:
time: 1000 us; the launch traced here: 984 us
  Pallas kernels  947 us (95%)
  local copies, waits for them, and re-layouts  37.3 us (4%)
    pallas_call x1, Pallas kernels, temporal_block(): pl.pallas_call(functools.partial(temporal_kernel, hd, n, axis), grid=(sha...  488 us
    pallas_call x1, Pallas kernels, spatial_block(): pl.pallas_call(functools.partial(spatial_kernel, hd, n, axis), grid=(fram...  458 us
    reshape x1, local copies, waits for them, and re-layouts, local_run(): w_qkv.reshape(L, C, 3 * heads * hd)  20.6 us

profile of v2, /device:TPU:113, one launch (start us, length us, event | category | flops | bytes accessed | tf_op | source)
XLA Modules:
  0.0 984.4 jit_solution(9435937223144850054)
XLA Ops:
  0.0 20.6 %copy.9.wqkv_h = bf16[2,1152,3456]{2,1,0:T(8,128)(2,1)} copy(bf16[2,1152,3456]{1,2,0:T(8,128)(2,1)} %bitcast.8) | data formatting | bytes 31850496 | tf_op jit(solution)/shard_map/reshape | solution.py:352
  20.6 458.3 %spatial.1.x_ref = bf16[128,64,1152]{2,1,0:T(8,128)(2,1)} custom-call(bf16[16,512,1152]{2,1,0:T(8,128)(2,1)} %bitcast.7, bf16[4,1152]{1,0:T(4,128)(2,1)} %gain_ref.3, bf16[4,1152]{1,0:T(4,128)(2,1)} %bias_ref.3, bf16[2,1152,3456]{2,1,0:T(8,128)(2,1)} %copy.9.wqkv_h, bf16[2,1152,1152]{2,1,0:T(8,128)(2,1)} %bitcast.5, bf16[2,1152,4608]{2,1,0:T(8,128)(2,1)} %wup_h.3, ...), custom_call_target="tpu_custom_call" | custom-call | tf_op jit(solution)/shard_map/spatial/pallas_call | solution.py:307
  478.9 488.2 %temporal.1 = bf16[16,512,1152]{2,1,0:T(8,128)(2,1)} custom-call(bf16[128,64,1152]{2,1,0:T(8,128)(2,1)} %spatial.1.x_ref, bf16[4,1152]{1,0:T(4,128)(2,1)} %gain_ref.3, bf16[4,1152]{1,0:T(4,128)(2,1)} %bias_ref.3, bf16[2,1152,3456]{2,1,0:T(8,128)(2,1)} %copy.9.wqkv_h, bf16[2,1152,1152]{2,1,0:T(8,128)(2,1)} %bitcast.6, bf16[2,1152,4608]{2,1,0:T(8,128)(2,1)} %wup_h.3, ...), custom_call_target="tpu_custom_call" | custom-call | tf_op jit(solution)/shard_map/temporal/pallas_call | solution.py:329
  967.1 16.7 %copy.12 = bf16[1,16,512,1152]{3,2,1,0:T(8,128)(2,1)} copy(bf16[1,16,512,1152]{3,2,1,0:T(8,128)(2,1)} %bitcast.4) | data formatting | bytes 37748736
